TPU v7x, 32 devices: a whole 2x2x4 slice. The times are simulated.
32 devices in a mesh: rep: 2 (over x), dp: 16 (over y, z, core).
Axes of the slice: x: 2, y: 2, z: 4, core: 2. Of those that a mesh axis runs over, the one named last changes fastest.
Arguments:
- g_w_gate: bfloat16 [32, 2, 1280, 3072], P(('rep', 'dp')), parts along dimension 0
- g_w_up: bfloat16 [32, 2, 1280, 3072], P(('rep', 'dp')), parts along dimension 0
- g_w_down: bfloat16 [32, 2, 3072, 1280], P(('rep', 'dp')), parts along dimension 0
- w_gate: bfloat16 [2, 1280, 3072], replicated
- w_up: bfloat16 [2, 1280, 3072], replicated
- w_down: bfloat16 [2, 3072, 1280], replicated
- m_w_gate: float32 [2, 1280, 3072], P(None, 'dp')
- m_w_up: float32 [2, 1280, 3072], P(None, 'dp')
- m_w_down: float32 [2, 3072, 1280], P(None, 'dp')
- v_w_gate: float32 [2, 1280, 3072], P(None, 'dp')
- v_w_up: float32 [2, 1280, 3072], P(None, 'dp')
- v_w_down: float32 [2, 3072, 1280], P(None, 'dp')
Outputs:
- output 1: bfloat16 [4, 1280, 3072], P('rep'), parts along dimension 0
- output 2: bfloat16 [4, 1280, 3072], P('rep'), parts along dimension 0
- output 3: bfloat16 [4, 3072, 1280], P('rep'), parts along dimension 0
- output 4: float32 [4, 1280, 3072], P('rep', 'dp'), parts along dimension 0
- output 5: float32 [4, 1280, 3072], P('rep', 'dp'), parts along dimension 0
- output 6: float32 [4, 3072, 1280], P('rep', 'dp'), parts along dimension 0
- output 7: float32 [4, 1280, 3072], P('rep', 'dp'), parts along dimension 0
- output 8: float32 [4, 1280, 3072], P('rep', 'dp'), parts along dimension 0
- output 9: float32 [4, 3072, 1280], P('rep', 'dp'), parts along dimension 0
There are 2 independent parts. A program takes and returns all parts, laid end to end along the dimension named above; an argument that names none is the same for every part.
All inputs are finite; a program needn't handle non-finite values.
Results may differ from a plain program's by a relative error of at most 0.022.
Values are sent between devices in bfloat16 or wider.
A program may use at most 2 GiB of HBM per device.

v0:
```python
import jax
import jax.numpy as jnp
from jax import lax
from jax.sharding import PartitionSpec as P


def adamw(w, m, v, g):
    m = 0.9 * m + 0.1 * g
    v = 0.95 * v + 0.05 * g * g
    step = m * lax.rsqrt(v + 1e-8) + 0.1 * w
    return (w - 0.02 * step).astype(jnp.bfloat16), m, v


def clipped(gradients, sum_of_squares, count):
    factor = jnp.minimum(1.0, 0.5 * lax.rsqrt(sum_of_squares / count + 1e-30))
    return [g * factor for g in gradients]


def solution(mesh):
    def step(*arrays):
        terms, weights, m, v = (arrays[i : i + 3] for i in (0, 3, 6, 9))
        gradients = [lax.psum_scatter(t[0], "dp", scatter_dimension=1, tiled=True).astype(jnp.float32) for t in terms]
        squares = lax.psum(sum(jnp.sum(g * g) for g in gradients), "dp")
        gradients = clipped(gradients, squares, lax.psum(1, "dp") * sum(g.size for g in gradients))
        me = lax.axis_index("dp")
        own = [lax.dynamic_slice_in_dim(w, me * one.shape[1], one.shape[1], 1).astype(jnp.float32) for w, one in zip(weights, m, strict=True)]
        new = [adamw(w, m, v, g) for w, m, v, g in zip(own, m, v, gradients, strict=True)]
        whole = [lax.all_gather(one[0], "dp", axis=1, tiled=True) for one in new]
        return (*whole, *(one[1] for one in new), *(one[2] for one in new))

    all_of, cut = P(None, None, None), P(None, "dp", None)
    return jax.shard_map(
        step,
        mesh=mesh,
        in_specs=(P(("rep", "dp"), None, None, None),) * 3 + (all_of,) * 3 + (cut,) * 6,
        out_specs=(P("rep", None, None),) * 3 + (P("rep", "dp", None),) * 6,
        check_vma=False,
    )
```

profile of v0, /device:TPU:0, one launch (start us, length us, event | category | flops | bytes accessed | tf_op | source)
XLA Modules:
  0.0 926.5 jit_solution(8459333657179808549)
XLA Ops:
  7.2 0.0 reduce-scatter.4.cloned.1.call-start
  7.2 0.7 reduce-scatter.4.cloned.1.call-update
  7.9 0.0 reduce-scatter.6.cloned.1.call-start
  8.0 0.7 reduce-scatter.6.cloned.1.call-update
  8.7 0.0 reduce-scatter.8.cloned.1.call-start
  8.7 0.7 reduce-scatter.8.cloned.1.call-update
  9.4 0.0 copy-start.3
  9.4 0.0 all-gather.8.cloned.1.call-start
  9.5 160.8 %reduce-scatter.4.cloned.1.call-done = bf16[2,80,3072]{2,1,0:T(8,128)(2,1)} async-done(((bf16[2,1280,3072]{2,1,0:T(8,128)(2,1)}), bf16[2,80,3072]{2,1,0:T(8,128)(2,1)}) %reduce-scatter.4.cloned.1.call-update) | async-done | bytes 983056 | tf_op jit(solution)/shard_map/reduce_scatter | solution.py:22
  170.3 2.3 fusion.9
  172.6 156.8 %reduce-scatter.6.cloned.1.call-done = bf16[2,80,3072]{2,1,0:T(8,128)(2,1)} async-done(((bf16[2,1280,3072]{2,1,0:T(8,128)(2,1)}), bf16[2,80,3072]{2,1,0:T(8,128)(2,1)}) %reduce-scatter.6.cloned.1.call-update) | async-done | bytes 983056 | tf_op jit(solution)/shard_map/reduce_scatter | solution.py:22
  329.4 2.3 fusion.10
  333.0 155.5 %reduce-scatter.8.cloned.1.call-done = bf16[2,192,1280]{2,1,0:T(8,128)(2,1)} async-done(((bf16[2,3072,1280]{2,1,0:T(8,128)(2,1)}), bf16[2,192,1280]{2,1,0:T(8,128)(2,1)}) %reduce-scatter.8.cloned.1.call-update) | async-done | bytes 983056 | tf_op jit(solution)/shard_map/reduce_scatter | solution.py:22
  488.6 2.3 fusion.11
  491.5 32.2 %psum.7 = f32[]{:T(128)} all-reduce(f32[]{:T(128)S(6)} %add.65), channel_id=1, replica_groups=mesh['rep'=2,'dp'=16] {'dp'}, use_global_device_ids=true, to_apply=%region_6.0 | all-reduce | flops 1 | bytes 8 | tf_op jit(solution)/shard_map/psum | solution.py:23
  524.5 5.0 fusion.17
  529.5 0.0 all-gather.8.cloned.1.call-update
  529.5 0.0 all-gather.4.cloned.1.call-start
  529.6 5.3 fusion.8
  534.9 0.0 all-gather.4.cloned.1.call-update
  535.0 0.0 all-gather.6.cloned.1.call-start
  535.0 5.3 fusion.14
  540.3 0.0 all-gather.6.cloned.1.call-update
  540.3 105.9 %all-gather.8.cloned.1.call-done = bf16[2,3072,1280]{2,1,0:T(8,128)(2,1)} async-done(((bf16[2,192,1280]{2,1,0:T(8,128)(2,1)}), bf16[2,3072,1280]{2,1,0:T(8,128)(2,1)}) %all-gather.8.cloned.1.call-update) | async-done | bytes 15728656 | tf_op jit(solution)/shard_map/all_gather | solution.py:28
  646.2 120.7 %all-gather.4.cloned.1.call-done = bf16[2,1280,3072]{2,1,0:T(8,128)(2,1)} async-done(((bf16[2,80,3072]{2,1,0:T(8,128)(2,1)}), bf16[2,1280,3072]{2,1,0:T(8,128)(2,1)}) %all-gather.4.cloned.1.call-update) | async-done | bytes 15728656 | tf_op jit(solution)/shard_map/all_gather | solution.py:28
  766.9 120.7 %all-gather.6.cloned.1.call-done = bf16[2,1280,3072]{2,1,0:T(8,128)(2,1)} async-done(((bf16[2,80,3072]{2,1,0:T(8,128)(2,1)}), bf16[2,1280,3072]{2,1,0:T(8,128)(2,1)}) %all-gather.6.cloned.1.call-update) | async-done | bytes 15728656 | tf_op jit(solution)/shard_map/all_gather | solution.py:28
  887.6 15.9 %copy.24 = bf16[2,1280,3072]{2,1,0:T(8,128)(2,1)} copy(bf16[2,1280,3072]{2,1,0:T(8,128)(2,1)} %all-gather.4.cloned.1.call-done) | data formatting | bytes 31457280
  903.4 8.0 copy.25
  911.4 0.0 slice-done.1
  911.4 1.3 slice-done.2
  912.7 1.1 slice-done.3
  913.9 5.8 copy.26
  (13 shorter events, 0.0 us)
Async XLA Ops:
  7.2 163.1 %reduce-scatter.4.cloned.1.call-start = ((), (), s32[]{:S(2)}) async-start(), calls=%async_computation.3 | async-start | bytes 16711680 | tf_op jit(solution)/shard_map/reduce_scatter | solution.py:22
  7.9 321.5 %reduce-scatter.6.cloned.1.call-start = ((), (), s32[]{:S(2)}) async-start(), calls=%async_computation.4 | async-start | bytes 16711680 | tf_op jit(solution)/shard_map/reduce_scatter | solution.py:22
  8.7 479.9 %reduce-scatter.8.cloned.1.call-start = ((), (), s32[]{:S(2)}) async-start(), calls=%async_computation.5 | async-start | bytes 16711680 | tf_op jit(solution)/shard_map/reduce_scatter | solution.py:22
  9.4 515.1 %copy-start.3 = (f32[2,192,1280]{2,1,0:T(8,128)S(1)}, f32[2,192,1280]{2,1,0:T(8,128)}, u32[]{:S(2)}) copy-start(f32[2,192,1280]{2,1,0:T(8,128)} %param.23) | copy-start | bytes 5898244
  9.4 636.8 %all-gather.8.cloned.1.call-start = ((), (), s32[]{:S(2)}) async-start(), calls=%async_computation.8 | async-start | bytes 16711680 | tf_op jit(solution)/shard_map/all_gather | solution.py:28
  524.5 5.1 copy-start.2
  529.5 237.4 %all-gather.4.cloned.1.call-start = ((), (), s32[]{:S(2)}) async-start(), calls=%async_computation.6 | async-start | bytes 16711680 | tf_op jit(solution)/shard_map/all_gather | solution.py:28
  529.6 5.4 copy-start.1
  535.0 352.6 %all-gather.6.cloned.1.call-start = ((), (), s32[]{:S(2)}) async-start(), calls=%async_computation.7 | async-start | bytes 16711680 | tf_op jit(solution)/shard_map/all_gather | solution.py:28
  887.6 15.9 %copy-start = (bf16[2,1280,3072]{2,1,0:T(8,128)(2,1)S(1)}, bf16[2,1280,3072]{2,1,0:T(8,128)(2,1)}, u32[]{:S(2)}) copy-start(bf16[2,1280,3072]{2,1,0:T(8,128)(2,1)} %all-gather.6.cloned.1.call-done) | copy-start | bytes 47185924
  887.6 23.8 %slice-start = ((s8[15728640]{0:T(1024)(128)(4,1)}), s8[4194304]{0:T(1024)(128)(4,1)S(1)}, s32[]{:S(2)}) async-start(s8[15728640]{0:T(1024)(128)(4,1)} %bitcast.6), calls=%async_computation.9 | async-start | bytes 8388608
  887.6 23.8 %slice-start.1 = ((s8[15728640]{0:T(1024)(128)(4,1)}), s8[4194304]{0:T(1024)(128)(4,1)S(1)}, s32[]{:S(2)}) async-start(s8[15728640]{0:T(1024)(128)(4,1)} %bitcast.6), calls=%async_computation.10 | async-start | bytes 8388608
  887.6 25.1 %slice-start.2 = ((s8[15728640]{0:T(1024)(128)(4,1)}), s8[4194304]{0:T(1024)(128)(4,1)S(1)}, s32[]{:S(2)}) async-start(s8[15728640]{0:T(1024)(128)(4,1)} %bitcast.6), calls=%async_computation.11 | async-start | bytes 8388608
  903.4 10.4 %slice-start.3 = ((s8[15728640]{0:T(1024)(128)(4,1)}), s8[3145728]{0:T(1024)(128)(4,1)S(1)}, s32[]{:S(2)}) async-start(s8[15728640]{0:T(1024)(128)(4,1)} %bitcast.6), calls=%async_computation.12 | async-start | bytes 6291456
Sparse Core Ops, SparseCore 0:
  12.1 158.1 reduce-scatter.3
  174.4 154.9 reduce-scatter.5
  333.5 154.9 reduce-scatter.7
  529.6 116.5 all-gather.7
  648.9 117.9 all-gather.3
  769.6 117.9 all-gather.5
where the time goes:
time: 927 us
  waiting for transfers between devices  823 us (89%)
  blocking collectives  32.2 us (3%)
  local copies, waits for them, and re-layouts  32.1 us (3%)
  other arithmetic  22.6 us (2%)
  between operations  16.8 us (2%)
    reduce_scatter x3, waiting for transfers between devices, step(): lax.psum_scatter(t[0], 'dp', scatter_dimension=1, tiled=True)  473 us
    all_gather x3, waiting for transfers between devices, step(): whole = [lax.all_gather(one[0], 'dp', axis=1, tiled=True) for one in new]  347 us
    psum x1, blocking collectives, step(): squares = lax.psum(sum((jnp.sum(g * g) for g in gradients)), 'dp')  32.2 us
    unnamed x19, local copies, waits for them, and re-layouts  32.1 us
  transfers between devices with their start and end apart: 6, of which 6 were waited for; matrix products, arithmetic and copies ran while one was open for 2% of the time, Pallas kernels for 0%

commit v1 on v0

v1 whole, which is shorter than its diff:
```python
import functools

import jax
import jax.numpy as jnp
from jax import lax
from jax.experimental import pallas as pl
from jax.experimental.pallas import tpu as pltpu
from jax.sharding import PartitionSpec as P

MESH = pl.DeviceIdType.MESH
CHIPS, DEVICES = 8, 16
PIECES = [(i, way) for i in range(3) for way in range(2)]


def adamw(w, m, v, g):
    m = 0.9 * m + 0.1 * g
    v = 0.95 * v + 0.05 * g * g
    step = m * lax.rsqrt(v + 1e-8) + 0.1 * w
    return (w - 0.02 * step).astype(jnp.bfloat16), m, v


def at(place):
    return place + lax.div(place, 4) * (11 - 2 * place)


def tiles(height, width):
    wide = 512 if width % 512 == 0 else 640
    return height // 16, [slice(k, k + wide) for k in range(0, width, wide)]


def kernel(count, g, w, m, v, whole, new_m, new_v, held, squares, own_sem, m_sem, v_sem, ring_send, ring_recv, pair_send, pair_recv, sq_send, sq_recv):
    rep, me = lax.axis_index("rep"), lax.axis_index("dp")
    chip, core = lax.div(me, 2), lax.rem(me, 2)
    place = at(chip)
    heights = [one.shape[1] for one in new_m]
    slots = [held[0].at[0], held[0].at[1], held[0].at[2], held[0].at[3], held[1].at[0], held[1].at[1]]

    def device(place, core):
        return 2 * at(lax.rem(place + 2 * CHIPS, CHIPS)) + core

    def block(way, step):
        return place - 1 - step if way == 0 else place + 1 + step

    def rows(i, owner):
        return pl.ds(pl.multiple_of(owner * heights[i], 16), heights[i])

    def ring(j, step, owner):
        i, way = PIECES[j]
        part = whole[i].at[way, rows(i, owner)]
        return pltpu.make_async_remote_copy(
            src_ref=part, dst_ref=part, send_sem=ring_send.at[step, j], recv_sem=ring_recv.at[step, j],
            device_id=(rep, device(place + 1 if way == 0 else place - 1, core)), device_id_type=MESH,
        )

    def pair(j, step, source, owner):
        i, way = PIECES[j]
        return pltpu.make_async_remote_copy(
            src_ref=source, dst_ref=whole[i].at[way, rows(i, owner)], send_sem=pair_send.at[step, j], recv_sem=pair_recv.at[step, j],
            device_id=(rep, 2 * chip + 1 - core), device_id_type=MESH,
        )

    def term(j, step):
        i, way = PIECES[j]
        owner = device(block(way, step), 1 - core)
        return pair(j, step, g[i].at[0, way, rows(i, owner)], owner)

    def own(j, step):
        i, way = PIECES[j]
        return pltpu.make_async_copy(g[i].at[0, way, rows(i, device(block(way, step), core))], slots[j], own_sem.at[j])

    def load_w(j):
        i, way = PIECES[j]
        return pltpu.make_async_copy(w[i].at[way, rows(i, me)], slots[j], own_sem.at[j])

    def load_m(j):
        i, way = PIECES[j]
        return pltpu.make_async_copy(m[i].at[way], new_m[i].at[way], m_sem.at[j])

    def load_v(j):
        i, way = PIECES[j]
        return pltpu.make_async_copy(v[i].at[way], new_v[i].at[way], v_sem.at[j])

    def add(j, step, first=False):
        i, way = PIECES[j]
        groups, columns = tiles(heights[i], whole[i].shape[2])
        mine = pl.multiple_of(device(block(way, step), core) * heights[i], 16)
        other = pl.multiple_of(device(block(way, step), 1 - core) * heights[i], 16)

        def group(r, _):
            for c in columns:
                total = slots[j][pl.ds(r * 16, 16), c].astype(jnp.float32) + whole[i][way, pl.ds(mine + r * 16, 16), c].astype(jnp.float32)
                if not first:
                    total = total + whole[i][way, pl.ds(other + r * 16, 16), c].astype(jnp.float32)
                whole[i][way, pl.ds(other + r * 16, 16), c] = total.astype(jnp.bfloat16)
            return 0

        lax.fori_loop(0, groups, group, 0)

    def last_add(j, so_far):
        i, way = PIECES[j]
        groups, columns = tiles(heights[i], whole[i].shape[2])
        mine = pl.multiple_of(me * heights[i], 16)
        other = pl.multiple_of((2 * chip + 1 - core) * heights[i], 16)

        def group(r, so_far):
            for c in columns:
                total = slots[j][pl.ds(r * 16, 16), c].astype(jnp.float32) + whole[i][way, pl.ds(mine + r * 16, 16), c].astype(jnp.float32)
                total = (total + whole[i][way, pl.ds(other + r * 16, 16), c].astype(jnp.float32)).astype(jnp.bfloat16)
                whole[i][way, pl.ds(mine + r * 16, 16), c] = total
                total = total.astype(jnp.float32)
                total = total * total
                for k in range(0, total.shape[1], 128):
                    so_far = so_far + total[:8, k : k + 128] + total[8:, k : k + 128]
            return so_far

        return lax.fori_loop(0, groups, group, so_far)

    def update(j, factor):
        i, way = PIECES[j]
        groups, columns = tiles(heights[i], whole[i].shape[2])
        mine = pl.multiple_of(me * heights[i], 16)

        def group(r, _):
            for c in columns:
                here = (way, pl.ds(r * 16, 16), c)
                there = (way, pl.ds(mine + r * 16, 16), c)
                gradient = whole[i][there].astype(jnp.float32) * factor
                new, new_m[i][here], new_v[i][here] = adamw(slots[j][pl.ds(r * 16, 16), c].astype(jnp.float32), new_m[i][here], new_v[i][here], gradient)
                whole[i][there] = new
            return 0

        lax.fori_loop(0, groups, group, 0)

    every = range(len(PIECES))
    for j in every:
        own(j, 0).start()
    barrier = pltpu.get_barrier_semaphore()
    for k in range(1, DEVICES):
        pl.semaphore_signal(barrier, inc=1, device_id=(rep, lax.rem(me + k, DEVICES)), device_id_type=MESH)
    pl.semaphore_wait(barrier, DEVICES - 1)

    for step in range(2):
        for j in every:
            term(j, step).start()
    for j in every:
        own(j, 0).wait()
        term(j, 0).wait_recv()
        add(j, 0, first=True)
        ring(j, 0, device(block(PIECES[j][1], 0), 1 - core)).start()
        own(j, 1).start()
    for j in every:
        load_m(j).start()
        load_v(j).start()

    def reduce_step(step, _):
        for j in every:
            term(j, step + 1).start()
        for j in every:
            owner = device(block(PIECES[j][1], step), 1 - core)
            own(j, step).wait()
            term(j, step).wait_recv()
            ring(j, step - 1, owner).wait_recv()
            add(j, step)
            ring(j, step, owner).start()
            own(j, step + 1).start()
            ring(j, step - 1, owner).wait_send()
            term(j, step - 1).wait_send()
        return 0

    lax.fori_loop(1, CHIPS - 1, reduce_step, 0)

    so_far = jnp.zeros((8, 128), jnp.float32)
    for j in every:
        own(j, CHIPS - 1).wait()
        term(j, CHIPS - 1).wait_recv()
        ring(j, CHIPS - 2, 2 * chip + 1 - core).wait_recv()
        so_far = last_add(j, so_far)
        load_w(j).start()
    for j in every:
        term(j, CHIPS - 2).wait_send()
        term(j, CHIPS - 1).wait_send()
        ring(j, CHIPS - 2, 2 * chip + 1 - core).wait_send()

    squares[me] = so_far

    def tell(k):
        return pltpu.make_async_remote_copy(
            src_ref=squares.at[me], dst_ref=squares.at[me], send_sem=sq_send.at[k], recv_sem=sq_recv.at[k],
            device_id=(rep, lax.rem(me + k, DEVICES)), device_id_type=MESH,
        )

    for k in range(1, DEVICES):
        tell(k).start()
    for j in every:
        load_m(j).wait()
        load_v(j).wait()
        load_w(j).wait()
    for k in range(1, DEVICES):
        tell(k).wait_recv()
    total = squares[0]
    for k in range(1, DEVICES):
        total = total + squares[k]
    total = jnp.sum(jnp.sum(total, axis=0, keepdims=True), axis=1, keepdims=True)
    factor = jnp.minimum(1.0, 0.5 * lax.rsqrt(total / count + 1e-30))

    def carried(j, step):
        return device(place - step if PIECES[j][1] == 0 else place + step, core)

    def on(j, step):
        return ring(j, step, carried(j, step))

    def across(j, step):
        i, way = PIECES[j]
        owner = carried(j, step)
        return pair(j, step, whole[i].at[way, rows(i, owner)], owner)

    for j in every:
        update(j, factor)
        on(j, 0).start()
        across(j, 0).start()

    def gather_step(step, _):
        for j in every:
            on(j, step - 1).wait_recv()
            on(j, step).start()
            across(j, step).start()
            on(j, step - 1).wait_send()
            across(j, step - 1).wait_send()
        return 0

    lax.fori_loop(1, CHIPS - 1, gather_step, 0)
    for j in every:
        on(j, CHIPS - 2).wait_recv()
        across(j, CHIPS - 1).start()
        on(j, CHIPS - 2).wait_send()
        across(j, CHIPS - 2).wait_send()
    for k in range(1, DEVICES):
        tell(k).wait_send()
    for j in every:
        across(j, CHIPS - 1).wait_send()

    def arrived(step, _):
        for j in every:
            across(j, step).wait_recv()
        return 0

    lax.fori_loop(0, CHIPS, arrived, 0)


def put_out(*refs):
    copies = [pltpu.make_async_copy(refs[k].at[layer], refs[9 + k].at[layer], refs[18].at[k, layer]) for k in range(9) for layer in range(2)]
    for copy in copies:
        copy.start()
    for copy in copies:
        copy.wait()


def body(count, *refs):
    groups = [refs[k : k + 3] for k in range(0, 21, 3)]
    kernel(count, *groups, refs[21:23], *refs[23:])


def solution(mesh):
    def step(*arrays):
        weights, moments = arrays[3:6], arrays[6:9]
        count = DEVICES * sum(one.size for one in moments)
        heights = [one.shape[1] for one in moments]
        widths = [one.shape[2] for one in moments]
        dma = pltpu.SemaphoreType.DMA
        out = [pltpu.VMEM(one.shape, jnp.bfloat16) for one in weights] + 2 * [pltpu.VMEM(one.shape, jnp.float32) for one in moments]
        done = pl.pallas_call(
            functools.partial(body, count),
            out_shape=out,
            in_specs=[pl.BlockSpec(memory_space=pltpu.HBM)] * 12,
            out_specs=[pl.BlockSpec(memory_space=pltpu.VMEM)] * 9,
            scratch_shapes=[
                pltpu.VMEM((4, heights[0], widths[0]), jnp.bfloat16),
                pltpu.VMEM((2, heights[2], widths[2]), jnp.bfloat16),
                pltpu.VMEM((DEVICES, 8, 128), jnp.float32),
                dma((6,)), dma((6,)), dma((6,)),
                dma((7, 6)), dma((7, 6)), dma((8, 6)), dma((8, 6)),
                dma((DEVICES,)), dma((DEVICES,)),
            ],
            compiler_params=pltpu.CompilerParams(collective_id=0, has_side_effects=True, vmem_limit_bytes=4 << 20),
            name="train_step",
        )(*arrays)
        return pl.pallas_call(
            put_out,
            out_shape=[jax.ShapeDtypeStruct(one.shape, one.dtype) for one in done],
            in_specs=[pl.BlockSpec(memory_space=pltpu.VMEM)] * 9,
            out_specs=[pl.BlockSpec(memory_space=pltpu.HBM)] * 9,
            scratch_shapes=[dma((9, 2))],
            compiler_params=pltpu.CompilerParams(vmem_limit_bytes=1 << 20),
            name="put_out",
        )(*[pltpu.with_memory_space_constraint(one, pltpu.VMEM) for one in done])

    all_of, cut = P(None, None, None), P(None, "dp", None)
    return jax.shard_map(
        step,
        mesh=mesh,
        in_specs=(P(("rep", "dp"), None, None, None),) * 3 + (all_of,) * 3 + (cut,) * 6,
        out_specs=(P("rep", None, None),) * 3 + (P("rep", "dp", None),) * 6,
        check_vma=False,
    )
```

time: 927 us -> 532 us (0.57)
  waiting for transfers between devices: 823 us -> 0 us
  Pallas kernels: 0 us -> 483 us
  blocking collectives: 32.2 us -> 0 us
  other arithmetic: 22.6 us -> 0 us
  between operations: 16.8 us -> 0.68 us
  local copies, waits for them, and re-layouts: 32.1 us -> 47.9 us
    pallas_call x0 -> x2, Pallas kernels: none -> 483 us  [the longest x1 464 us: step(): pl.pallas_call(functools.partial(body, count), out_shape=out, in_specs=[p...]
    reduce_scatter x3 -> x0, waiting for transfers between devices: 473 us -> none  [step(): lax.psum_scatter(t[0], 'dp', scatter_dimension=1, tiled=True)]
    all_gather x3 -> x0, waiting for transfers between devices: 347 us -> none  [step(): whole = [lax.all_gather(one[0], 'dp', axis=1, tiled=True) for one in new]]
    psum x1 -> x0, blocking collectives: 32.2 us -> none  [step(): squares = lax.psum(sum((jnp.sum(g * g) for g in gradients)), 'dp')]
    unnamed x19 -> x32, local copies, waits for them, and re-layouts: 32.1 us -> 47.9 us
    convert_element_type x3 -> x0, other arithmetic: 15.6 us -> none  [adamw(): return ((w - 0.02 * step).astype(jnp.bfloat16), m, v)]
  transfers between devices with their start and end apart: 6 -> 0, of which waited for: 6 -> 0; matrix products, arithmetic and copies ran while one was open for 2% -> 0% of each run, Pallas kernels for 0% -> 0%
where the time goes in v1:
time: 532 us; the launch traced here: 531 us
  Pallas kernels  483 us (91%)
  local copies, waits for them, and re-layouts  47.9 us (9%)
    pallas_call x1, Pallas kernels, step(): pl.pallas_call(functools.partial(body, count), out_shape=out, in_specs=[p...  464 us
    unnamed x32, local copies, waits for them, and re-layouts  47.9 us
    pallas_call x1, Pallas kernels, step(): pl.pallas_call(put_out, out_shape=[jax.ShapeDtypeStruct(one.shape, one.dt...  18.8 us

profile of v1, /device:TPU:0, one launch (start us, length us, event | category | flops | bytes accessed | tf_op | source)
XLA Modules:
  0.0 531.2 jit_solution(1158036939158860745)
XLA Ops:
  0.6 463.9 %train_step.1 = (bf16[2,1280,3072]{2,1,0:T(8,128)(2,1)S(1)}, bf16[2,1280,3072]{2,1,0:T(8,128)(2,1)S(1)}, bf16[2,3072,1280]{2,1,0:T(8,128)(2,1)S(1)}, f32[2,80,30...) custom-call(bf16[1,2,1280,3072]{3,2,1,0:T(8,128)(2,1)} %refs_0_.1, ...), custom_call_target="tpu_custom_call" | custom-call | tf_op jit(solution)/shard_map/train_step/pallas_call | solution.py:271
  464.5 0.0 copy-start
  464.5 5.8 %copy-done = bf16[2,1280,3072]{2,1,0:T(8,128)(2,1)} copy-done((bf16[2,1280,3072]{2,1,0:T(8,128)(2,1)}, bf16[2,1280,3072]{2,1,0:T(8,128)(2,1)S(1)}, u32[]{:S(2)}) %copy-start) | copy-done | bytes 15728664
  470.3 0.0 copy-start.2
  470.3 5.8 %copy-done.2 = bf16[2,1280,3072]{2,1,0:T(8,128)(2,1)} copy-done((bf16[2,1280,3072]{2,1,0:T(8,128)(2,1)}, bf16[2,1280,3072]{2,1,0:T(8,128)(2,1)S(1)}, u32[]{:S(2)}) %copy-start.2) | copy-done | bytes 15728664
  476.1 0.0 copy-start.4
  476.1 5.8 %copy-done.4 = bf16[2,3072,1280]{2,1,0:T(8,128)(2,1)} copy-done((bf16[2,3072,1280]{2,1,0:T(8,128)(2,1)}, bf16[2,3072,1280]{2,1,0:T(8,128)(2,1)S(1)}, u32[]{:S(2)}) %copy-start.4) | copy-done | bytes 15728664
  481.9 0.0 copy-start.6
  482.0 1.3 copy-done.6
  483.2 0.0 copy-start.8
  483.2 1.3 copy-done.8
  484.5 0.0 copy-start.10
  484.5 1.3 copy-done.10
  485.8 0.0 copy-start.12
  485.8 1.3 copy-done.12
  487.0 0.0 copy-start.14
  487.0 1.3 copy-done.14
  488.3 0.0 copy-start.1
  488.3 5.5 %copy-done.1 = bf16[2,1280,3072]{2,1,0:T(8,128)(2,1)S(1)} copy-done((bf16[2,1280,3072]{2,1,0:T(8,128)(2,1)S(1)}, bf16[2,1280,3072]{2,1,0:T(8,128)(2,1)}, u32[]{:S(2)}) %copy-start.1) | copy-done | bytes 15728664
  493.8 0.0 copy-start.3
  493.8 5.5 %copy-done.3 = bf16[2,1280,3072]{2,1,0:T(8,128)(2,1)S(1)} copy-done((bf16[2,1280,3072]{2,1,0:T(8,128)(2,1)S(1)}, bf16[2,1280,3072]{2,1,0:T(8,128)(2,1)}, u32[]{:S(2)}) %copy-start.3) | copy-done | bytes 15728664
  499.2 0.0 copy-start.5
  499.3 5.5 %copy-done.5 = bf16[2,3072,1280]{2,1,0:T(8,128)(2,1)S(1)} copy-done((bf16[2,3072,1280]{2,1,0:T(8,128)(2,1)S(1)}, bf16[2,3072,1280]{2,1,0:T(8,128)(2,1)}, u32[]{:S(2)}) %copy-start.5) | copy-done | bytes 15728664
  504.7 0.0 copy-start.7
  504.7 1.5 copy-done.7
  506.3 0.0 copy-start.9
  506.3 1.5 copy-done.9
  507.8 0.0 copy-start.11
  507.8 1.5 copy-done.11
  509.4 1.5 copy-done.13
  510.9 1.5 copy-done.15
  512.5 18.8 %put_out.1 = (bf16[2,1280,3072]{2,1,0:T(8,128)(2,1)}, bf16[2,1280,3072]{2,1,0:T(8,128)(2,1)}, bf16[2,3072,1280]{2,1,0:T(8,128)(2,1)}, f32[2,80,3072]{2,1,0:T(8,1...) custom-call(bf16[2,1280,3072]{2,1,0:T(8,128)(2,1)S(1)} %copy-done.1,, ...), custom_call_target="tpu_custom_call" | custom-call | tf_op jit(solution)/shard_map/put_out/pallas_call | solution.py:287
  (2 shorter events, 0.0 us)
Async XLA Ops:
  464.5 5.8 %copy-start = (bf16[2,1280,3072]{2,1,0:T(8,128)(2,1)}, bf16[2,1280,3072]{2,1,0:T(8,128)(2,1)S(1)}, u32[]{:S(2)}) copy-start(bf16[2,1280,3072]{2,1,0:T(8,128)(2,1)S(1)} %get-tuple-element.18.refs_0_) | copy-start | bytes 47185924
  470.3 5.8 %copy-start.2 = (bf16[2,1280,3072]{2,1,0:T(8,128)(2,1)}, bf16[2,1280,3072]{2,1,0:T(8,128)(2,1)S(1)}, u32[]{:S(2)}) copy-start(bf16[2,1280,3072]{2,1,0:T(8,128)(2,1)S(1)} %get-tuple-element.19.refs_1_) | copy-start | bytes 47185924
  476.1 5.8 %copy-start.4 = (bf16[2,3072,1280]{2,1,0:T(8,128)(2,1)}, bf16[2,3072,1280]{2,1,0:T(8,128)(2,1)S(1)}, u32[]{:S(2)}) copy-start(bf16[2,3072,1280]{2,1,0:T(8,128)(2,1)S(1)} %get-tuple-element.20.refs_2_) | copy-start | bytes 47185924
  481.9 1.3 copy-start.6
  483.2 1.3 copy-start.8
  484.5 1.3 copy-start.10
  485.8 1.3 copy-start.12
  487.0 1.3 copy-start.14
  488.3 5.5 %copy-start.1 = (bf16[2,1280,3072]{2,1,0:T(8,128)(2,1)S(1)}, bf16[2,1280,3072]{2,1,0:T(8,128)(2,1)}, u32[]{:S(2)}) copy-start(bf16[2,1280,3072]{2,1,0:T(8,128)(2,1)} %copy-done) | copy-start | bytes 47185924
  493.8 5.5 %copy-start.3 = (bf16[2,1280,3072]{2,1,0:T(8,128)(2,1)S(1)}, bf16[2,1280,3072]{2,1,0:T(8,128)(2,1)}, u32[]{:S(2)}) copy-start(bf16[2,1280,3072]{2,1,0:T(8,128)(2,1)} %copy-done.2) | copy-start | bytes 47185924
  499.2 5.5 %copy-start.5 = (bf16[2,3072,1280]{2,1,0:T(8,128)(2,1)S(1)}, bf16[2,3072,1280]{2,1,0:T(8,128)(2,1)}, u32[]{:S(2)}) copy-start(bf16[2,3072,1280]{2,1,0:T(8,128)(2,1)} %copy-done.4) | copy-start | bytes 47185924
  504.7 1.5 copy-start.7
  506.3 1.5 copy-start.9
  507.8 1.5 copy-start.11
  509.4 1.5 copy-start.13
  510.9 1.5 copy-start.15

commit v2 on v1

--- a/solution.py
+++ b/solution.py
@@ -290,7 +290,7 @@
             in_specs=[pl.BlockSpec(memory_space=pltpu.VMEM)] * 9,
             out_specs=[pl.BlockSpec(memory_space=pltpu.HBM)] * 9,
             scratch_shapes=[dma((9, 2))],
-            compiler_params=pltpu.CompilerParams(vmem_limit_bytes=1 << 20),
+            compiler_params=pltpu.CompilerParams(vmem_limit_bytes=4 << 20),
             name="put_out",
         )(*[pltpu.with_memory_space_constraint(one, pltpu.VMEM) for one in done])
 

time: 532 us -> 483 us (0.908)
  local copies, waits for them, and re-layouts: 47.9 us -> 0 us
    unnamed x32 -> x0, local copies, waits for them, and re-layouts: 47.9 us -> none
where the time goes in v2:
time: 483 us
  Pallas kernels  483 us (100%)
    pallas_call x1, Pallas kernels, step(): pl.pallas_call(functools.partial(body, count), out_shape=out, in_specs=[p...  464 us
    pallas_call x1, Pallas kernels, step(): pl.pallas_call(put_out, out_shape=[jax.ShapeDtypeStruct(one.shape, one.dt...  18.8 us

profile of v2, /device:TPU:0, one launch (start us, length us, event | category | flops | bytes accessed | tf_op | source)
XLA Modules:
  0.0 483.3 jit_solution(8508319093709695464)
XLA Ops:
  0.6 463.9 %train_step.1 = (bf16[2,1280,3072]{2,1,0:T(8,128)(2,1)S(1)}, bf16[2,1280,3072]{2,1,0:T(8,128)(2,1)S(1)}, bf16[2,3072,1280]{2,1,0:T(8,128)(2,1)S(1)}, f32[2,80,30...) custom-call(bf16[1,2,1280,3072]{3,2,1,0:T(8,128)(2,1)} %refs_0_.1, ...), custom_call_target="tpu_custom_call" | custom-call | tf_op jit(solution)/shard_map/train_step/pallas_call | solution.py:271
  464.5 18.8 %put_out.1 = (bf16[2,1280,3072]{2,1,0:T(8,128)(2,1)}, bf16[2,1280,3072]{2,1,0:T(8,128)(2,1)}, bf16[2,3072,1280]{2,1,0:T(8,128)(2,1)}, f32[2,80,3072]{2,1,0:T(8,1...) custom-call(bf16[2,1280,3072]{2,1,0:T(8,128)(2,1)S(1)} %get-tuple-el, ...), custom_call_target="tpu_custom_call" | custom-call | tf_op jit(solution)/shard_map/put_out/pallas_call | solution.py:287

commit v3 on v2

--- a/solution.py
+++ b/solution.py
@@ -9,6 +9,8 @@
 
 MESH = pl.DeviceIdType.MESH
 CHIPS, DEVICES = 8, 16
+FIRST = ((0, 2), (2, 5))
+ORDER = [(0, FIRST[0]), (1, FIRST[0]), (0, FIRST[1]), (1, FIRST[1]), (2, None), (3, None), (4, None), (5, None)]
 PIECES = [(i, way) for i in range(3) for way in range(2)]
 
 
@@ -41,28 +43,30 @@
     def block(way, step):
         return place - 1 - step if way == 0 else place + 1 + step
 
-    def rows(i, owner):
-        return pl.ds(pl.multiple_of(owner * heights[i], 16), heights[i])
-
-    def ring(j, step, owner):
-        i, way = PIECES[j]
-        part = whole[i].at[way, rows(i, owner)]
+    def rows(i, owner, span=None):
+        low, high = span or (0, heights[i] // 16)
+        return pl.ds(pl.multiple_of(owner * heights[i] + 16 * low, 16), 16 * (high - low))
+
+    def ring(j, step, owner, span=None):
+        i, way = PIECES[j]
+        part = whole[i].at[way, rows(i, owner, span)]
         return pltpu.make_async_remote_copy(
             src_ref=part, dst_ref=part, send_sem=ring_send.at[step, j], recv_sem=ring_recv.at[step, j],
             device_id=(rep, device(place + 1 if way == 0 else place - 1, core)), device_id_type=MESH,
         )
 
-    def pair(j, step, source, owner):
-        i, way = PIECES[j]
+    def pair(j, step, source, owner, span=None):
+        i, way = PIECES[j]
+        arrival = CHIPS if span in FIRST[1:] else step
         return pltpu.make_async_remote_copy(
-            src_ref=source, dst_ref=whole[i].at[way, rows(i, owner)], send_sem=pair_send.at[step, j], recv_sem=pair_recv.at[step, j],
+            src_ref=source, dst_ref=whole[i].at[way, rows(i, owner, span)], send_sem=pair_send.at[step, j], recv_sem=pair_recv.at[arrival, j],
             device_id=(rep, 2 * chip + 1 - core), device_id_type=MESH,
         )
 
-    def term(j, step):
+    def term(j, step, span=None):
         i, way = PIECES[j]
         owner = device(block(way, step), 1 - core)
-        return pair(j, step, g[i].at[0, way, rows(i, owner)], owner)
+        return pair(j, step, g[i].at[0, way, rows(i, owner, span)], owner, span)
 
     def own(j, step):
         i, way = PIECES[j]
@@ -80,7 +84,7 @@
         i, way = PIECES[j]
         return pltpu.make_async_copy(v[i].at[way], new_v[i].at[way], v_sem.at[j])
 
-    def add(j, step, first=False):
+    def add(j, step, first=False, span=None):
         i, way = PIECES[j]
         groups, columns = tiles(heights[i], whole[i].shape[2])
         mine = pl.multiple_of(device(block(way, step), core) * heights[i], 16)
@@ -94,7 +98,7 @@
                 whole[i][way, pl.ds(other + r * 16, 16), c] = total.astype(jnp.bfloat16)
             return 0
 
-        lax.fori_loop(0, groups, group, 0)
+        lax.fori_loop(*(span or (0, groups)), group, 0)
 
     def last_add(j, so_far):
         i, way = PIECES[j]
@@ -115,7 +119,7 @@
 
         return lax.fori_loop(0, groups, group, so_far)
 
-    def update(j, factor):
+    def update(j, factor, span=None):
         i, way = PIECES[j]
         groups, columns = tiles(heights[i], whole[i].shape[2])
         mine = pl.multiple_of(me * heights[i], 16)
@@ -129,24 +133,26 @@
                 whole[i][there] = new
             return 0
 
-        lax.fori_loop(0, groups, group, 0)
+        lax.fori_loop(*(span or (0, groups)), group, 0)
 
     every = range(len(PIECES))
     for j in every:
         own(j, 0).start()
     barrier = pltpu.get_barrier_semaphore()
-    for k in range(1, DEVICES):
-        pl.semaphore_signal(barrier, inc=1, device_id=(rep, lax.rem(me + k, DEVICES)), device_id_type=MESH)
-    pl.semaphore_wait(barrier, DEVICES - 1)
-
-    for step in range(2):
-        for j in every:
-            term(j, step).start()
-    for j in every:
-        own(j, 0).wait()
-        term(j, 0).wait_recv()
-        add(j, 0, first=True)
-        ring(j, 0, device(block(PIECES[j][1], 0), 1 - core)).start()
+    for peer in (2 * chip + 1 - core, device(place + 1, core), device(place - 1, core)):
+        pl.semaphore_signal(barrier, inc=1, device_id=(rep, peer), device_id_type=MESH)
+    pl.semaphore_wait(barrier, 3)
+
+    for j, span in ORDER:
+        term(j, 0, span).start()
+    for j, span in ORDER:
+        if span not in FIRST[1:]:
+            own(j, 0).wait()
+        term(j, 0, span).wait_recv()
+        add(j, 0, first=True, span=span)
+        ring(j, 0, device(block(PIECES[j][1], 0), 1 - core), span).start()
+    for j in every:
+        term(j, 1).start()
         own(j, 1).start()
     for j in every:
         load_m(j).start()
@@ -214,10 +220,11 @@
         owner = carried(j, step)
         return pair(j, step, whole[i].at[way, rows(i, owner)], owner)
 
-    for j in every:
-        update(j, factor)
-        on(j, 0).start()
-        across(j, 0).start()
+    for j, span in ORDER:
+        update(j, factor, span)
+        ring(j, 0, me, span).start()
+        if span != FIRST[0]:
+            across(j, 0).start()
 
     def gather_step(step, _):
         for j in every:
@@ -278,7 +285,7 @@
                 pltpu.VMEM((2, heights[2], widths[2]), jnp.bfloat16),
                 pltpu.VMEM((DEVICES, 8, 128), jnp.float32),
                 dma((6,)), dma((6,)), dma((6,)),
-                dma((7, 6)), dma((7, 6)), dma((8, 6)), dma((8, 6)),
+                dma((7, 6)), dma((7, 6)), dma((8, 6)), dma((9, 6)),
                 dma((DEVICES,)), dma((DEVICES,)),
             ],
             compiler_params=pltpu.CompilerParams(collective_id=0, has_side_effects=True, vmem_limit_bytes=4 << 20),

time: 483 us -> 481 us (level)
  no operation moved by 1% of the time
where the time goes in v3:
time: 481 us
  Pallas kernels  480 us (100%)
    pallas_call x1, Pallas kernels, step(): pl.pallas_call(functools.partial(body, count), out_shape=out, in_specs=[p...  462 us
    pallas_call x1, Pallas kernels, step(): pl.pallas_call(put_out, out_shape=[jax.ShapeDtypeStruct(one.shape, one.dt...  18.8 us

profile of v3, /device:TPU:0, one launch (start us, length us, event | category | flops | bytes accessed | tf_op | source)
XLA Modules:
  0.0 481.0 jit_solution(14225968303983310256)
XLA Ops:
  0.6 461.6 %train_step.1 = (bf16[2,1280,3072]{2,1,0:T(8,128)(2,1)S(1)}, bf16[2,1280,3072]{2,1,0:T(8,128)(2,1)S(1)}, bf16[2,3072,1280]{2,1,0:T(8,128)(2,1)S(1)}, f32[2,80,30...) custom-call(bf16[1,2,1280,3072]{3,2,1,0:T(8,128)(2,1)} %refs_0_.1, ...), custom_call_target="tpu_custom_call" | custom-call | tf_op jit(solution)/shard_map/train_step/pallas_call | solution.py:278
  462.2 18.8 %put_out.1 = (bf16[2,1280,3072]{2,1,0:T(8,128)(2,1)}, bf16[2,1280,3072]{2,1,0:T(8,128)(2,1)}, bf16[2,3072,1280]{2,1,0:T(8,128)(2,1)}, f32[2,80,3072]{2,1,0:T(8,1...) custom-call(bf16[2,1280,3072]{2,1,0:T(8,128)(2,1)S(1)} %get-tuple-el, ...), custom_call_target="tpu_custom_call" | custom-call | tf_op jit(solution)/shard_map/put_out/pallas_call | solution.py:294

commit v4 on v3

--- a/solution.py
+++ b/solution.py
@@ -30,7 +30,7 @@
     return height // 16, [slice(k, k + wide) for k in range(0, width, wide)]
 
 
-def kernel(count, g, w, m, v, whole, new_m, new_v, held, squares, own_sem, m_sem, v_sem, ring_send, ring_recv, pair_send, pair_recv, sq_send, sq_recv):
+def kernel(count, g, w, m, v, whole, new_m, new_v, last, held, squares, last_sem, own_sem, m_sem, v_sem, ring_send, ring_recv, pair_send, pair_recv, sq_send, sq_recv):
     rep, me = lax.axis_index("rep"), lax.axis_index("dp")
     chip, core = lax.div(me, 2), lax.rem(me, 2)
     place = at(chip)
@@ -235,23 +235,59 @@
             across(j, step - 1).wait_send()
         return 0
 
-    lax.fori_loop(1, CHIPS - 1, gather_step, 0)
-    for j in every:
+    lax.fori_loop(1, CHIPS - 2, gather_step, 0)
+
+    def hand_out(j):
+        i, way = PIECES[j]
+        return pltpu.make_async_copy(whole[i].at[way, rows(i, carried(j, CHIPS - 2))], last[way].at[i], last_sem.at[j])
+
+    for j in every:
+        on(j, CHIPS - 3).wait_recv()
+        if j < 4:
+            hand_out(j).start()
+        else:
+            on(j, CHIPS - 2).start()
+        across(j, CHIPS - 2).start()
+        on(j, CHIPS - 3).wait_send()
+        across(j, CHIPS - 3).wait_send()
+    for j in every[4:]:
         on(j, CHIPS - 2).wait_recv()
         across(j, CHIPS - 1).start()
         on(j, CHIPS - 2).wait_send()
-        across(j, CHIPS - 2).wait_send()
     for k in range(1, DEVICES):
         tell(k).wait_send()
     for j in every:
-        across(j, CHIPS - 1).wait_send()
+        across(j, CHIPS - 2).wait_send()
+        if j < 4:
+            hand_out(j).wait()
+        else:
+            across(j, CHIPS - 1).wait_send()
+            across(j, CHIPS - 1).wait_recv()
 
     def arrived(step, _):
         for j in every:
             across(j, step).wait_recv()
         return 0
 
-    lax.fori_loop(0, CHIPS, arrived, 0)
+    lax.fori_loop(0, CHIPS - 1, arrived, 0)
+
+
+def put_last(*refs):
+    arrived, out, sem = refs[2:6], refs[6:8], refs[8]
+    me = lax.axis_index("dp")
+    chip, core = lax.div(me, 2), lax.rem(me, 2)
+    height = arrived[0].shape[1]
+    copies = []
+    for k, one in enumerate(arrived):
+        way = k % 2
+        place = lax.rem(at(chip) + (1 if way == 0 else CHIPS - 1), CHIPS)
+        owner = 2 * at(place) + (core if k < 2 else 1 - core)
+        there = pl.ds(pl.multiple_of(owner * height, 16), height)
+        copies += [pltpu.make_async_copy(one.at[i], out[i].at[way, there], sem.at[k, i]) for i in range(2)]
+    for copy in copies:
+        copy.start()
+    for copy in copies:
+        copy.wait()
 
 
 def put_out(*refs):
@@ -264,7 +300,7 @@
 
 def body(count, *refs):
     groups = [refs[k : k + 3] for k in range(0, 21, 3)]
-    kernel(count, *groups, refs[21:23], *refs[23:])
+    kernel(count, *groups, refs[21:23], refs[23:25], *refs[25:])
 
 
 def solution(mesh):
@@ -275,31 +311,52 @@
         widths = [one.shape[2] for one in moments]
         dma = pltpu.SemaphoreType.DMA
         out = [pltpu.VMEM(one.shape, jnp.bfloat16) for one in weights] + 2 * [pltpu.VMEM(one.shape, jnp.float32) for one in moments]
-        done = pl.pallas_call(
+        piece = pltpu.HBM((2, *moments[0].shape[1:]), jnp.bfloat16)
+        *done, up, down = pl.pallas_call(
             functools.partial(body, count),
-            out_shape=out,
+            out_shape=[*out, piece, piece],
             in_specs=[pl.BlockSpec(memory_space=pltpu.HBM)] * 12,
-            out_specs=[pl.BlockSpec(memory_space=pltpu.VMEM)] * 9,
+            out_specs=[pl.BlockSpec(memory_space=pltpu.VMEM)] * 9 + [pl.BlockSpec(memory_space=pltpu.HBM)] * 2,
             scratch_shapes=[
                 pltpu.VMEM((4, heights[0], widths[0]), jnp.bfloat16),
                 pltpu.VMEM((2, heights[2], widths[2]), jnp.bfloat16),
                 pltpu.VMEM((DEVICES, 8, 128), jnp.float32),
-                dma((6,)), dma((6,)), dma((6,)),
+                dma((4,)), dma((6,)), dma((6,)), dma((6,)),
                 dma((7, 6)), dma((7, 6)), dma((8, 6)), dma((9, 6)),
                 dma((DEVICES,)), dma((DEVICES,)),
             ],
             compiler_params=pltpu.CompilerParams(collective_id=0, has_side_effects=True, vmem_limit_bytes=4 << 20),
             name="train_step",
         )(*arrays)
-        return pl.pallas_call(
+        ring = [place + place // 4 * (11 - 2 * place) for place in range(CHIPS)]
+        hop = [(2 * ring[k] + core, 2 * ring[(k + 1) % CHIPS] + core) for k in range(CHIPS) for core in range(2)]
+        up = lax.ppermute(up, "dp", hop)
+        down = lax.ppermute(down, "dp", [(b, a) for a, b in hop])
+        in_hbm, in_vmem = pl.BlockSpec(memory_space=pltpu.HBM), pl.BlockSpec(memory_space=pltpu.VMEM)
+        gate, up_w, *rest = pl.pallas_call(
             put_out,
             out_shape=[jax.ShapeDtypeStruct(one.shape, one.dtype) for one in done],
-            in_specs=[pl.BlockSpec(memory_space=pltpu.VMEM)] * 9,
-            out_specs=[pl.BlockSpec(memory_space=pltpu.HBM)] * 9,
+            in_specs=[in_vmem] * 9,
+            out_specs=[in_hbm] * 9,
             scratch_shapes=[dma((9, 2))],
             compiler_params=pltpu.CompilerParams(vmem_limit_bytes=4 << 20),
+            cost_estimate=pl.CostEstimate(flops=500_000_000, bytes_accessed=60_000_000, transcendentals=0),
             name="put_out",
         )(*[pltpu.with_memory_space_constraint(one, pltpu.VMEM) for one in done])
+        up, down, rest[-1] = lax.optimization_barrier((up, down, rest[-1]))
+        partner = [(k, k + 1 - 2 * (k % 2)) for k in range(DEVICES)]
+        across = [lax.ppermute(one, "dp", partner) for one in (up, down)]
+        gate, up_w = pl.pallas_call(
+            put_last,
+            out_shape=[jax.ShapeDtypeStruct(one.shape, one.dtype) for one in (gate, up_w)],
+            in_specs=[in_hbm] * 2 + [in_vmem] * 4,
+            out_specs=[in_hbm] * 2,
+            scratch_shapes=[dma((4, 2))],
+            input_output_aliases={0: 0, 1: 1},
+            compiler_params=pltpu.CompilerParams(vmem_limit_bytes=16 << 20),
+            name="put_last",
+        )(gate, up_w, up, down, *across)
+        return (gate, up_w, *rest)
 
     all_of, cut = P(None, None, None), P(None, "dp", None)
     return jax.shard_map(

time: 481 us -> 474 us (0.985)
  Pallas kernels: 480 us -> 462 us
  waiting for transfers between devices: 0 us -> 7.79 us
    pallas_call x1 -> x2, Pallas kernels: 462 us -> 444 us  [the longest x1 442 us: step(): pl.pallas_call(functools.partial(body, count), out_shape=[*out, piece, pi...]
    ppermute x0 -> x4, waiting for transfers between devices: none -> 7.79 us  [the longest x2 3.46 us: step(): across = [lax.ppermute(one, 'dp', partner) for one in (up, down)]]
  transfers between devices with their start and end apart: 0 -> 4, of which waited for: 0 -> 4; matrix products, arithmetic and copies ran while one was open for 0% -> 0% of each run, Pallas kernels for 0% -> 4%
where the time goes in v4:
time: 474 us; the launch traced here: 473 us
  Pallas kernels  462 us (97%)
  waiting for transfers between devices  7.79 us (2%)
    pallas_call x1, Pallas kernels, step(): pl.pallas_call(functools.partial(body, count), out_shape=[*out, piece, pi...  442 us
    pallas_call x1, Pallas kernels, step(): pl.pallas_call(put_out, out_shape=[jax.ShapeDtypeStruct(one.shape, one.dt...  18.8 us
  transfers between devices with their start and end apart: 4, of which 4 were waited for; matrix products, arithmetic and copies ran while one was open for 0% of the time, Pallas kernels for 4%

profile of v4, /device:TPU:0, one launch (start us, length us, event | category | flops | bytes accessed | tf_op | source)
XLA Modules:
  0.0 473.4 jit_solution(3115204104884051067)
XLA Ops:
  0.6 441.6 %train_step.1 = (bf16[2,1280,3072]{2,1,0:T(8,128)(2,1)S(1)}, bf16[2,1280,3072]{2,1,0:T(8,128)(2,1)S(1)}, bf16[2,3072,1280]{2,1,0:T(8,128)(2,1)S(1)}, f32[2,80,30...) custom-call(bf16[1,2,1280,3072]{3,2,1,0:T(8,128)(2,1)} %refs_0_.1, ...), custom_call_target="tpu_custom_call" | custom-call | tf_op jit(solution)/shard_map/train_step/pallas_call | solution.py:315
  442.2 1.4 collective-permute-start
  443.6 0.6 collective-permute-start.1
  444.3 18.8 %put_out.1 = (bf16[2,1280,3072]{2,1,0:T(8,128)(2,1)}, bf16[2,1280,3072]{2,1,0:T(8,128)(2,1)}, bf16[2,3072,1280]{2,1,0:T(8,128)(2,1)}, f32[2,80,3072]{2,1,0:T(8,1...) custom-call(bf16[2,1280,3072]{2,1,0:T(8,128)(2,1)S(1)} %get-tuple-el, ...), custom_call_target="tpu_custom_call" | custom-call | flops 500000000 | bytes 60000000 | tf_op jit(solution)/shard_map/put_out/pallas_call | solution.py:336
  463.1 3.2 collective-permute-done.refs_2_
  466.3 1.1 collective-permute-done.1.refs_3_
  467.4 0.0 collective-permute-start.2
  467.4 0.5 collective-permute-start.3
  467.9 2.1 collective-permute-done.2.refs_4_
  470.0 1.4 collective-permute-done.3.refs_5_
  471.4 2.0 put_last.1
Async XLA Ops:
  442.2 24.1 %collective-permute-start = (bf16[2,80,3072]{2,1,0:T(8,128)(2,1)}, bf16[2,80,3072]{2,1,0:T(8,128)(2,1)S(1)}, u32[]{:S(2)}, u32[]{:S(2)}) collective-permute-start(bf16[2,80,3072]{2,1,0:T(8,128)(2,1)} %get-tuple-element.45), channel_id=1, source_target_pairs={{0,2},{1,3},{2,4},{3,5},{4,6},{5,7},{6,14},{7,15},{14,12},{15,13},... | collective-permute-start | bytes 2949128 | tf_op jit(solution)/shard_map/ppermute | solution.py:333
  443.6 23.8 %collective-permute-start.1 = (bf16[2,80,3072]{2,1,0:T(8,128)(2,1)}, bf16[2,80,3072]{2,1,0:T(8,128)(2,1)S(1)}, u32[]{:S(2)}, u32[]{:S(2)}) collective-permute-start(bf16[2,80,3072]{2,1,0:T(8,128)(2,1)} %get-tuple-element.46), channel_id=1, source_target_pairs={{2,0},{3,1},{4,2},{5,3},{6,4},{7,5},{14,6},{15,7},{12,14},{13,15},... | collective-permute-start | bytes 2949128 | tf_op jit(solution)/shard_map/ppermute | solution.py:334
  467.4 2.6 collective-permute-start.2
  467.4 4.0 collective-permute-start.3

commit v5 on v4

--- a/solution.py
+++ b/solution.py
@@ -179,12 +179,12 @@
     for j in every:
         own(j, CHIPS - 1).wait()
         term(j, CHIPS - 1).wait_recv()
+        term(j, CHIPS - 2).wait_send()
+        term(j, CHIPS - 1).wait_send()
         ring(j, CHIPS - 2, 2 * chip + 1 - core).wait_recv()
         so_far = last_add(j, so_far)
         load_w(j).start()
     for j in every:
-        term(j, CHIPS - 2).wait_send()
-        term(j, CHIPS - 1).wait_send()
         ring(j, CHIPS - 2, 2 * chip + 1 - core).wait_send()
 
     squares[me] = so_far
@@ -226,6 +226,9 @@
         if span != FIRST[0]:
             across(j, 0).start()
 
+    for k in range(1, DEVICES):
+        tell(k).wait_send()
+
     def gather_step(step, _):
         for j in every:
             on(j, step - 1).wait_recv()
@@ -233,13 +236,14 @@
             across(j, step).start()
             on(j, step - 1).wait_send()
             across(j, step - 1).wait_send()
+            across(j, step - 1).wait_recv()
         return 0
 
     lax.fori_loop(1, CHIPS - 2, gather_step, 0)
 
     def hand_out(j):
         i, way = PIECES[j]
-        return pltpu.make_async_copy(whole[i].at[way, rows(i, carried(j, CHIPS - 2))], last[way].at[i], last_sem.at[j])
+        return pltpu.make_async_copy(whole[i].at[way, rows(i, carried(j, CHIPS - 2))], last[j], last_sem.at[j])
 
     for j in every:
         on(j, CHIPS - 3).wait_recv()
@@ -250,40 +254,33 @@
         across(j, CHIPS - 2).start()
         on(j, CHIPS - 3).wait_send()
         across(j, CHIPS - 3).wait_send()
+        across(j, CHIPS - 3).wait_recv()
     for j in every[4:]:
         on(j, CHIPS - 2).wait_recv()
         across(j, CHIPS - 1).start()
         on(j, CHIPS - 2).wait_send()
-    for k in range(1, DEVICES):
-        tell(k).wait_send()
     for j in every:
         across(j, CHIPS - 2).wait_send()
+        across(j, CHIPS - 2).wait_recv()
         if j < 4:
             hand_out(j).wait()
-        else:
-            across(j, CHIPS - 1).wait_send()
-            across(j, CHIPS - 1).wait_recv()
-
-    def arrived(step, _):
-        for j in every:
-            across(j, step).wait_recv()
-        return 0
-
-    lax.fori_loop(0, CHIPS - 1, arrived, 0)
+    for j in every[4:]:
+        across(j, CHIPS - 1).wait_send()
+        across(j, CHIPS - 1).wait_recv()
 
 
 def put_last(*refs):
-    arrived, out, sem = refs[2:6], refs[6:8], refs[8]
+    arrived, out, sem = refs[2:10], refs[10:12], refs[12]
     me = lax.axis_index("dp")
     chip, core = lax.div(me, 2), lax.rem(me, 2)
-    height = arrived[0].shape[1]
+    height = arrived[0].shape[0]
     copies = []
     for k, one in enumerate(arrived):
-        way = k % 2
+        i, way = PIECES[k % 4]
         place = lax.rem(at(chip) + (1 if way == 0 else CHIPS - 1), CHIPS)
-        owner = 2 * at(place) + (core if k < 2 else 1 - core)
+        owner = 2 * at(place) + (core if k < 4 else 1 - core)
         there = pl.ds(pl.multiple_of(owner * height, 16), height)
-        copies += [pltpu.make_async_copy(one.at[i], out[i].at[way, there], sem.at[k, i]) for i in range(2)]
+        copies.append(pltpu.make_async_copy(one, out[i].at[way, there], sem.at[k]))
     for copy in copies:
         copy.start()
     for copy in copies:
@@ -300,7 +297,7 @@
 
 def body(count, *refs):
     groups = [refs[k : k + 3] for k in range(0, 21, 3)]
-    kernel(count, *groups, refs[21:23], refs[23:25], *refs[25:])
+    kernel(count, *groups, refs[21:25], refs[25:27], *refs[27:])
 
 
 def solution(mesh):
@@ -311,12 +308,12 @@
         widths = [one.shape[2] for one in moments]
         dma = pltpu.SemaphoreType.DMA
         out = [pltpu.VMEM(one.shape, jnp.bfloat16) for one in weights] + 2 * [pltpu.VMEM(one.shape, jnp.float32) for one in moments]
-        piece = pltpu.HBM((2, *moments[0].shape[1:]), jnp.bfloat16)
-        *done, up, down = pl.pallas_call(
+        piece = pltpu.HBM(moments[0].shape[1:], jnp.bfloat16)
+        *done, gate0, gate1, up0, up1 = pl.pallas_call(
             functools.partial(body, count),
-            out_shape=[*out, piece, piece],
+            out_shape=[*out, piece, piece, piece, piece],
             in_specs=[pl.BlockSpec(memory_space=pltpu.HBM)] * 12,
-            out_specs=[pl.BlockSpec(memory_space=pltpu.VMEM)] * 9 + [pl.BlockSpec(memory_space=pltpu.HBM)] * 2,
+            out_specs=[pl.BlockSpec(memory_space=pltpu.VMEM)] * 9 + [pl.BlockSpec(memory_space=pltpu.HBM)] * 4,
             scratch_shapes=[
                 pltpu.VMEM((4, heights[0], widths[0]), jnp.bfloat16),
                 pltpu.VMEM((2, heights[2], widths[2]), jnp.bfloat16),
@@ -330,8 +327,8 @@
         )(*arrays)
         ring = [place + place // 4 * (11 - 2 * place) for place in range(CHIPS)]
         hop = [(2 * ring[k] + core, 2 * ring[(k + 1) % CHIPS] + core) for k in range(CHIPS) for core in range(2)]
-        up = lax.ppermute(up, "dp", hop)
-        down = lax.ppermute(down, "dp", [(b, a) for a, b in hop])
+        back = [(b, a) for a, b in hop]
+        last = [lax.ppermute(one, "dp", way) for one, way in ((gate0, hop), (gate1, back), (up0, hop), (up1, back))]
         in_hbm, in_vmem = pl.BlockSpec(memory_space=pltpu.HBM), pl.BlockSpec(memory_space=pltpu.VMEM)
         gate, up_w, *rest = pl.pallas_call(
             put_out,
@@ -343,19 +340,20 @@
             cost_estimate=pl.CostEstimate(flops=500_000_000, bytes_accessed=60_000_000, transcendentals=0),
             name="put_out",
         )(*[pltpu.with_memory_space_constraint(one, pltpu.VMEM) for one in done])
-        up, down, rest[-1] = lax.optimization_barrier((up, down, rest[-1]))
+        last[0], last[1], rest[-1] = lax.optimization_barrier((last[0], last[1], rest[-1]))
+        last[2], last[3], rest[-2] = lax.optimization_barrier((last[2], last[3], rest[-2]))
         partner = [(k, k + 1 - 2 * (k % 2)) for k in range(DEVICES)]
-        across = [lax.ppermute(one, "dp", partner) for one in (up, down)]
+        across = [lax.ppermute(one, "dp", partner) for one in last]
         gate, up_w = pl.pallas_call(
             put_last,
             out_shape=[jax.ShapeDtypeStruct(one.shape, one.dtype) for one in (gate, up_w)],
-            in_specs=[in_hbm] * 2 + [in_vmem] * 4,
+            in_specs=[in_hbm] * 2 + [in_vmem] * 8,
             out_specs=[in_hbm] * 2,
-            scratch_shapes=[dma((4, 2))],
+            scratch_shapes=[dma((8,))],
             input_output_aliases={0: 0, 1: 1},
             compiler_params=pltpu.CompilerParams(vmem_limit_bytes=16 << 20),
             name="put_last",
-        )(gate, up_w, up, down, *across)
+        )(gate, up_w, *last, *across)
         return (gate, up_w, *rest)
 
     all_of, cut = P(None, None, None), P(None, "dp", None)

time: 474 us -> 472 us (level)
  transfers between devices with their start and end apart: 4 -> 8, of which waited for: 4 -> 4; matrix products, arithmetic and copies ran while one was open for 0% -> 0% of each run, Pallas kernels for 4% -> 4%
where the time goes in v5:
time: 472 us
  Pallas kernels  462 us (98%)
  starting transfers between devices  5.18 us (1%)
    pallas_call x1, Pallas kernels, step(): pl.pallas_call(functools.partial(body, count), out_shape=[*out, piece, pi...  441 us
    pallas_call x1, Pallas kernels, step(): pl.pallas_call(put_out, out_shape=[jax.ShapeDtypeStruct(one.shape, one.dt...  18.8 us
  transfers between devices with their start and end apart: 8, of which 4 were waited for; matrix products, arithmetic and copies ran while one was open for 0% of the time, Pallas kernels for 4%

profile of v5, /device:TPU:0, one launch (start us, length us, event | category | flops | bytes accessed | tf_op | source)
XLA Modules:
  0.0 471.8 jit_solution(12383521701818918766)
XLA Ops:
  0.6 441.5 %train_step.1 = (bf16[2,1280,3072]{2,1,0:T(8,128)(2,1)S(1)}, bf16[2,1280,3072]{2,1,0:T(8,128)(2,1)S(1)}, bf16[2,3072,1280]{2,1,0:T(8,128)(2,1)S(1)}, f32[2,80,30...) custom-call(bf16[1,2,1280,3072]{3,2,1,0:T(8,128)(2,1)} %refs_0_.1, ...), custom_call_target="tpu_custom_call" | custom-call | tf_op jit(solution)/shard_map/train_step/pallas_call | solution.py:312
  442.1 1.4 collective-permute-start
  443.5 0.6 collective-permute-start.1
  444.2 1.4 collective-permute-start.2
  445.6 0.6 collective-permute-start.3
  446.2 18.8 %put_out.1 = (bf16[2,1280,3072]{2,1,0:T(8,128)(2,1)}, bf16[2,1280,3072]{2,1,0:T(8,128)(2,1)}, bf16[2,3072,1280]{2,1,0:T(8,128)(2,1)}, f32[2,80,3072]{2,1,0:T(8,1...) custom-call(bf16[2,1280,3072]{2,1,0:T(8,128)(2,1)S(1)} %get-tuple-el, ...), custom_call_target="tpu_custom_call" | custom-call | flops 500000000 | bytes 60000000 | tf_op jit(solution)/shard_map/put_out/pallas_call | solution.py:333
  465.0 0.0 collective-permute-done.refs_2_
  465.0 0.0 collective-permute-done.1.refs_3_
  465.0 0.1 collective-permute-start.4
  465.1 0.5 collective-permute-start.5
  465.6 0.6 collective-permute-done.2.refs_4_
  466.2 1.1 collective-permute-done.3.refs_5_
  467.3 0.0 collective-permute-start.6
  467.3 0.5 collective-permute-start.7
  467.8 0.0 collective-permute-done.4.refs_6_
  467.8 0.0 collective-permute-done.5.refs_7_
  467.8 1.3 collective-permute-done.6.refs_8_
  469.2 0.7 collective-permute-done.7.refs_9_
  469.9 2.0 put_last.1
Async XLA Ops:
  442.1 22.9 %collective-permute-start = (bf16[80,3072]{1,0:T(8,128)(2,1)}, bf16[80,3072]{1,0:T(8,128)(2,1)S(1)}, u32[]{:S(2)}, u32[]{:S(2)}) collective-permute-start(bf16[80,3072]{1,0:T(8,128)(2,1)} %get-tuple-element.50), channel_id=1, source_target_pairs={{0,2},{1,3},{2,4},{3,5},{4,6},{5,7},{6,14},{7,15},{14,12},{15,13},... | collective-permute-start | bytes 1474568 | tf_op jit(solution)/shard_map/ppermute | solution.py:331
  443.5 21.5 %collective-permute-start.1 = (bf16[80,3072]{1,0:T(8,128)(2,1)}, bf16[80,3072]{1,0:T(8,128)(2,1)S(1)}, u32[]{:S(2)}, u32[]{:S(2)}) collective-permute-start(bf16[80,3072]{1,0:T(8,128)(2,1)} %get-tuple-element.51), channel_id=1, source_target_pairs={{2,0},{3,1},{4,2},{5,3},{6,4},{7,5},{14,6},{15,7},{12,14},{13,15},... | collective-permute-start | bytes 1474568 | tf_op jit(solution)/shard_map/ppermute | solution.py:331
  444.2 22.0 %collective-permute-start.2 = (bf16[80,3072]{1,0:T(8,128)(2,1)}, bf16[80,3072]{1,0:T(8,128)(2,1)S(1)}, u32[]{:S(2)}, u32[]{:S(2)}) collective-permute-start(bf16[80,3072]{1,0:T(8,128)(2,1)} %get-tuple-element.55), channel_id=1, source_target_pairs={{0,2},{1,3},{2,4},{3,5},{4,6},{5,7},{6,14},{7,15},{14,12},{15,13},... | collective-permute-start | bytes 1474568 | tf_op jit(solution)/shard_map/ppermute | solution.py:331
  445.6 21.7 %collective-permute-start.3 = (bf16[80,3072]{1,0:T(8,128)(2,1)}, bf16[80,3072]{1,0:T(8,128)(2,1)S(1)}, u32[]{:S(2)}, u32[]{:S(2)}) collective-permute-start(bf16[80,3072]{1,0:T(8,128)(2,1)} %get-tuple-element.56), channel_id=1, source_target_pairs={{2,0},{3,1},{4,2},{5,3},{6,4},{7,5},{14,6},{15,7},{12,14},{13,15},... | collective-permute-start | bytes 1474568 | tf_op jit(solution)/shard_map/ppermute | solution.py:331
  465.0 2.8 collective-permute-start.4
  465.1 2.7 collective-permute-start.5
  467.3 1.9 collective-permute-start.6
  467.3 2.6 collective-permute-start.7

commit v6 on v5

--- a/solution.py
+++ b/solution.py
@@ -9,7 +9,7 @@
 
 MESH = pl.DeviceIdType.MESH
 CHIPS, DEVICES = 8, 16
-FIRST = ((0, 2), (2, 5))
+FIRST = ((0, 1), (1, 5))
 ORDER = [(0, FIRST[0]), (1, FIRST[0]), (0, FIRST[1]), (1, FIRST[1]), (2, None), (3, None), (4, None), (5, None)]
 PIECES = [(i, way) for i in range(3) for way in range(2)]
 

time: 472 us -> 472 us (level)
  no operation moved by 1% of the time
where the time goes in v6:
time: 472 us; the launch traced here: 471 us
  Pallas kernels  462 us (98%)
  starting transfers between devices  5.18 us (1%)
    pallas_call x1, Pallas kernels, step(): pl.pallas_call(functools.partial(body, count), out_shape=[*out, piece, pi...  441 us
    pallas_call x1, Pallas kernels, step(): pl.pallas_call(put_out, out_shape=[jax.ShapeDtypeStruct(one.shape, one.dt...  18.8 us
  transfers between devices with their start and end apart: 8, of which 4 were waited for; matrix products, arithmetic and copies ran while one was open for 0% of the time, Pallas kernels for 4%

profile of v6, /device:TPU:0, one launch (start us, length us, event | category | flops | bytes accessed | tf_op | source)
XLA Modules:
  0.0 471.4 jit_solution(3306779209416109531)
XLA Ops:
  0.6 441.1 %train_step.1 = (bf16[2,1280,3072]{2,1,0:T(8,128)(2,1)S(1)}, bf16[2,1280,3072]{2,1,0:T(8,128)(2,1)S(1)}, bf16[2,3072,1280]{2,1,0:T(8,128)(2,1)S(1)}, f32[2,80,30...) custom-call(bf16[1,2,1280,3072]{3,2,1,0:T(8,128)(2,1)} %refs_0_.1, ...), custom_call_target="tpu_custom_call" | custom-call | tf_op jit(solution)/shard_map/train_step/pallas_call | solution.py:312
  441.8 1.3 collective-permute-start
  443.1 0.7 collective-permute-start.1
  443.8 1.3 collective-permute-start.2
  445.1 0.7 collective-permute-start.3
  445.9 18.8 %put_out.1 = (bf16[2,1280,3072]{2,1,0:T(8,128)(2,1)}, bf16[2,1280,3072]{2,1,0:T(8,128)(2,1)}, bf16[2,3072,1280]{2,1,0:T(8,128)(2,1)}, f32[2,80,3072]{2,1,0:T(8,1...) custom-call(bf16[2,1280,3072]{2,1,0:T(8,128)(2,1)S(1)} %get-tuple-el, ...), custom_call_target="tpu_custom_call" | custom-call | flops 500000000 | bytes 60000000 | tf_op jit(solution)/shard_map/put_out/pallas_call | solution.py:333
  464.6 0.0 collective-permute-done.refs_2_
  464.7 0.0 collective-permute-done.1.refs_3_
  464.7 0.1 collective-permute-start.4
  464.7 0.5 collective-permute-start.5
  465.2 0.6 collective-permute-done.2.refs_4_
  465.9 1.0 collective-permute-done.3.refs_5_
  466.9 0.0 collective-permute-start.6
  466.9 0.5 collective-permute-start.7
  467.4 0.0 collective-permute-done.4.refs_6_
  467.4 0.0 collective-permute-done.5.refs_7_
  467.4 1.3 collective-permute-done.6.refs_8_
  468.7 0.7 collective-permute-done.7.refs_9_
  469.4 2.0 put_last.1
Async XLA Ops:
  441.8 22.9 %collective-permute-start = (bf16[80,3072]{1,0:T(8,128)(2,1)}, bf16[80,3072]{1,0:T(8,128)(2,1)S(1)}, u32[]{:S(2)}, u32[]{:S(2)}) collective-permute-start(bf16[80,3072]{1,0:T(8,128)(2,1)} %get-tuple-element.50), channel_id=1, source_target_pairs={{0,2},{1,3},{2,4},{3,5},{4,6},{5,7},{6,14},{7,15},{14,12},{15,13},... | collective-permute-start | bytes 1474568 | tf_op jit(solution)/shard_map/ppermute | solution.py:331
  443.1 21.5 %collective-permute-start.1 = (bf16[80,3072]{1,0:T(8,128)(2,1)}, bf16[80,3072]{1,0:T(8,128)(2,1)S(1)}, u32[]{:S(2)}, u32[]{:S(2)}) collective-permute-start(bf16[80,3072]{1,0:T(8,128)(2,1)} %get-tuple-element.51), channel_id=1, source_target_pairs={{2,0},{3,1},{4,2},{5,3},{6,4},{7,5},{14,6},{15,7},{12,14},{13,15},... | collective-permute-start | bytes 1474568 | tf_op jit(solution)/shard_map/ppermute | solution.py:331
  443.8 22.0 %collective-permute-start.2 = (bf16[80,3072]{1,0:T(8,128)(2,1)}, bf16[80,3072]{1,0:T(8,128)(2,1)S(1)}, u32[]{:S(2)}, u32[]{:S(2)}) collective-permute-start(bf16[80,3072]{1,0:T(8,128)(2,1)} %get-tuple-element.55), channel_id=1, source_target_pairs={{0,2},{1,3},{2,4},{3,5},{4,6},{5,7},{6,14},{7,15},{14,12},{15,13},... | collective-permute-start | bytes 1474568 | tf_op jit(solution)/shard_map/ppermute | solution.py:331
  445.1 21.7 %collective-permute-start.3 = (bf16[80,3072]{1,0:T(8,128)(2,1)}, bf16[80,3072]{1,0:T(8,128)(2,1)S(1)}, u32[]{:S(2)}, u32[]{:S(2)}) collective-permute-start(bf16[80,3072]{1,0:T(8,128)(2,1)} %get-tuple-element.56), channel_id=1, source_target_pairs={{2,0},{3,1},{4,2},{5,3},{6,4},{7,5},{14,6},{15,7},{12,14},{13,15},... | collective-permute-start | bytes 1474568 | tf_op jit(solution)/shard_map/ppermute | solution.py:331
  464.7 2.7 collective-permute-start.4
  464.7 2.6 collective-permute-start.5
  466.9 1.9 collective-permute-start.6
  466.9 2.6 collective-permute-start.7
